TPU v7x, 128 devices: a whole 4x4x4 slice. The times are simulated.
128 devices in a mesh: dp: 32 (over x, y, z_lo), seq: 4 (over z_hi, core).
Axes of the slice: x: 4, y: 4, z: 4 (z_hi: 2, z_lo: 2; z = z_hi * 2 + z_lo), core: 2. Of those that a mesh axis runs over, the one named last changes fastest.
Arguments:
- qkv: bfloat16 [64, 1024, 4608], P('dp', 'seq'), may hold values from -20.4 to 20.4
- gate: float32 [64, 3072], P('dp'), may hold values from 0.5 to 2.5
- cotangent: bfloat16 [64, 1024, 3072], P('dp', 'seq'), may hold values from -6 to 6
- out_weight: bfloat16 [1536, 3072], replicated, may hold values from -0.15625 to 0.15625
- clip_lengths: int32 [64], replicated, may hold values from 1 to 768, as said below
- text_lengths: int32 [64], replicated, may hold values from 1 to 256, as said below
- plan: int32 [32], replicated, may hold values from 0 to 31, as said below
Outputs:
- mixed: bfloat16 [64, 1024, 3072], P('dp', 'seq')
- gate_grad: float32 [64, 3072], P('dp')
- weight_grad: float32 [1536, 3072], P(None, ('dp', 'seq'))
- qkv_grad: bfloat16 [64, 1024, 4608], P('dp', 'seq')
Inputs may be any that keep to these rules, and one draw needn't show every extreme that they name: clip_lengths[c] counts the live video positions of source clip c = 2 g + s (group g, slot s); some clip has exactly 768. text_lengths[c] counts the live text positions of source clip c; some clip has exactly 256. plan is a permutation of 0 to 31: the second clip of group g becomes the second clip of group plan[g].
All inputs are finite; a program needn't handle non-finite values.
Results may differ from a plain program's by a relative error of at most 0.011.
Values may be sent and summed in bfloat16 or wider, within the bound.
No kernel may reach another device: no remote copies, remote signals or barrier semaphores. Data moves between devices by JAX's collectives and lax.ppermute only.
A program may use at most 128 MiB of HBM per device.

v0:
```python
import jax
import jax.numpy as jnp
from jax import lax
from jax.sharding import PartitionSpec as P

HD = 128
TXT = 256
BLOCK = 512
NEGATIVE = -1e30


def from_everyone(x, axis):
    copies = jnp.broadcast_to(x, (lax.axis_size(axis), *x.shape))
    return lax.all_to_all(copies, axis, split_axis=0, concat_axis=0, tiled=True)


def taken_together(x, axis):
    everything = from_everyone(x, axis)
    return jnp.sum(everything, axis=0)


def allowed_rows(offset, count, text_len, video_len):
    places = offset + jnp.arange(count, dtype=jnp.int32)
    return (places < text_len) | (places >= TXT) & (places < TXT + video_len)


def move_in(block_rows, inverse):
    groups = lax.axis_size("dp")
    portions = block_rows.reshape(groups, block_rows.shape[0] // groups, block_rows.shape[1])
    spread = lax.all_to_all(portions, "dp", split_axis=0, concat_axis=0, tiled=True)
    arranged = jnp.take(spread, inverse, axis=0)
    landed = lax.all_to_all(arranged, "dp", split_axis=0, concat_axis=0, tiled=True)
    return landed.reshape(block_rows.shape)


def move_out(block_rows, plan):
    groups = lax.axis_size("dp")
    portions = block_rows.reshape(groups, block_rows.shape[0] // groups, block_rows.shape[1])
    spread = lax.all_to_all(portions, "dp", split_axis=0, concat_axis=0, tiled=True)
    arranged = jnp.take(spread, plan, axis=0)
    landed = lax.all_to_all(arranged, "dp", split_axis=0, concat_axis=0, tiled=True)
    return landed.reshape(block_rows.shape)


def to_heads(tokens, seq_ways):
    clip_count, row_count, full_width = tokens.shape
    local_width = full_width // (3 * seq_ways)
    parted = tokens.reshape(clip_count, row_count, 3, seq_ways, local_width)
    exchanged = lax.all_to_all(parted, "seq", split_axis=3, concat_axis=1, tiled=True)
    return exchanged.reshape(clip_count, row_count * seq_ways, 3, local_width)


def block_scores(query_rows, key_rows, query_ok, key_ok, score_scale):
    scores = (
        jnp.einsum("qhd,khd->hqk", query_rows, key_rows, preferred_element_type=jnp.float32)
        * score_scale
    )
    live_pairs = query_ok[None, :, None] & key_ok[None, None, :]
    return (scores, live_pairs)


def attend(queries, keys_all, values_all, text_len, video_len, score_scale):
    seq_len, head_count, head_dim = queries.shape
    block_count = (TXT + video_len + BLOCK - 1) // BLOCK

    def query_step(query_block, built):
        results, log_totals = built
        offset = query_block * BLOCK
        query_rows = lax.dynamic_slice_in_dim(queries, offset, BLOCK, 0)
        query_ok = allowed_rows(offset, BLOCK, text_len, video_len)

        def scored(key_block):
            key_offset = key_block * BLOCK
            key_rows = lax.dynamic_slice_in_dim(keys_all, key_offset, BLOCK, 0)
            key_ok = allowed_rows(key_offset, BLOCK, text_len, video_len)
            scores, live_pairs = block_scores(query_rows, key_rows, query_ok, key_ok, score_scale)
            return (scores, live_pairs, key_offset)

        def stats_step(key_block, running):
            row_peak, row_total = running
            scores, live_pairs, key_offset = scored(key_block)
            masked = jnp.where(live_pairs, scores, NEGATIVE)
            new_peak = jnp.maximum(row_peak, jnp.max(masked, axis=-1))
            row_total = row_total * jnp.exp(row_peak - new_peak) + jnp.sum(
                jnp.exp(masked - new_peak[..., None]), axis=-1
            )
            return (new_peak, row_total)

        start_peak = jnp.full((head_count, BLOCK), NEGATIVE, jnp.float32)
        row_peak, row_total = lax.fori_loop(
            0, block_count, stats_step, (start_peak, jnp.zeros((head_count, BLOCK), jnp.float32))
        )
        log_total = row_peak + jnp.log(row_total)

        def value_step(key_block, partial_sums):
            scores, live_pairs, key_offset = scored(key_block)
            probs_low = jnp.exp(
                jnp.where(live_pairs, scores - log_total[..., None], NEGATIVE)
            ).astype(jnp.bfloat16)
            value_rows = lax.dynamic_slice_in_dim(values_all, key_offset, BLOCK, 0)
            return partial_sums + jnp.einsum(
                "hqk,khd->qhd", probs_low, value_rows, preferred_element_type=jnp.float32
            )

        partial_sums = lax.fori_loop(
            0, block_count, value_step, jnp.zeros((BLOCK, head_count, head_dim), jnp.float32)
        )
        results = lax.dynamic_update_slice_in_dim(
            results, partial_sums.astype(jnp.bfloat16), offset, 0
        )
        log_totals = lax.dynamic_update_slice_in_dim(log_totals, log_total, offset, 1)
        return (results, log_totals)

    initial = (
        jnp.zeros((seq_len, head_count, head_dim), jnp.bfloat16),
        jnp.zeros((head_count, seq_len), jnp.float32),
    )
    return lax.fori_loop(0, block_count, query_step, initial)


def attend_back(
    queries, keys_all, values_all, results, d_results, log_totals, text_len, video_len, score_scale
):
    seq_len, head_count, head_dim = queries.shape
    block_count = (TXT + video_len + BLOCK - 1) // BLOCK
    row_dots_all = jnp.einsum("qhd,qhd->hq", d_results, results, preferred_element_type=jnp.float32)

    def query_step(query_block, gradients):
        grad_q, grad_k, grad_v = gradients
        offset = query_block * BLOCK
        query_rows = lax.dynamic_slice_in_dim(queries, offset, BLOCK, 0)
        d_rows = lax.dynamic_slice_in_dim(d_results, offset, BLOCK, 0)
        query_ok = allowed_rows(offset, BLOCK, text_len, video_len)
        log_total = lax.dynamic_slice_in_dim(log_totals, offset, BLOCK, 1)
        row_dots = lax.dynamic_slice_in_dim(row_dots_all, offset, BLOCK, 1)

        def key_step(key_block, inner_state):
            q_sums, grad_k, grad_v = inner_state
            key_offset = key_block * BLOCK
            key_rows = lax.dynamic_slice_in_dim(keys_all, key_offset, BLOCK, 0)
            value_rows = lax.dynamic_slice_in_dim(values_all, key_offset, BLOCK, 0)
            key_ok = allowed_rows(key_offset, BLOCK, text_len, video_len)
            scores, live_pairs = block_scores(query_rows, key_rows, query_ok, key_ok, score_scale)
            probabilities = jnp.exp(jnp.where(live_pairs, scores - log_total[..., None], NEGATIVE))
            probs_low = probabilities.astype(jnp.bfloat16)
            d_probs = jnp.einsum(
                "qhd,khd->hqk", d_rows, value_rows, preferred_element_type=jnp.float32
            )
            d_scores = (probabilities * (d_probs - row_dots[..., None])).astype(jnp.bfloat16)
            q_sums = q_sums + jnp.einsum(
                "hqk,khd->qhd", d_scores, key_rows, preferred_element_type=jnp.float32
            )
            k_part = jnp.einsum(
                "hqk,qhd->khd", d_scores, query_rows, preferred_element_type=jnp.float32
            )
            v_part = jnp.einsum(
                "hqk,qhd->khd", probs_low, d_rows, preferred_element_type=jnp.float32
            )
            grad_k = lax.dynamic_update_slice_in_dim(
                grad_k,
                lax.dynamic_slice_in_dim(grad_k, key_offset, BLOCK, 0) + k_part,
                key_offset,
                0,
            )
            grad_v = lax.dynamic_update_slice_in_dim(
                grad_v,
                lax.dynamic_slice_in_dim(grad_v, key_offset, BLOCK, 0) + v_part,
                key_offset,
                0,
            )
            return (q_sums, grad_k, grad_v)

        q_start = jnp.zeros((BLOCK, head_count, head_dim), jnp.float32)
        q_sums, grad_k, grad_v = lax.fori_loop(0, block_count, key_step, (q_start, grad_k, grad_v))
        grad_q = lax.dynamic_update_slice_in_dim(grad_q, q_sums, offset, 0)
        return (grad_q, grad_k, grad_v)

    zero_grad = jnp.zeros((seq_len, head_count, head_dim), jnp.float32)
    grad_q, grad_k, grad_v = lax.fori_loop(
        0, block_count, query_step, (zero_grad, zero_grad, zero_grad)
    )
    return (
        (grad_q * score_scale).astype(jnp.bfloat16),
        (grad_k * score_scale).astype(jnp.bfloat16),
        grad_v.astype(jnp.bfloat16),
    )


def body(qkv, gate, cotangent, out_weight, clip_lengths, text_lengths, plan):
    groups = lax.axis_size("dp")
    seq_ways = lax.axis_size("seq")
    group_index = lax.axis_index("dp")
    seq_index = lax.axis_index("seq")
    ordinal = jnp.arange(groups, dtype=jnp.int32)
    inverse = jnp.sum(jnp.where(plan[None, :] == ordinal[:, None], ordinal[None, :], 0), axis=1)
    home_clip = 2 * group_index
    head_width = out_weight.shape[0]
    local_width = head_width // seq_ways
    head_count = local_width // HD
    row_count = cotangent.shape[1]
    score_scale = HD ** (-0.5)
    arrived = move_in(qkv[1], inverse)
    working = jnp.stack([qkv[0], arrived])
    clip_ids = (home_clip, 2 * inverse[group_index] + 1)
    spread_heads = to_heads(working, seq_ways)
    seq_len = spread_heads.shape[1]
    video_lens = [clip_lengths[clip_id] for clip_id in clip_ids]
    text_lens = [text_lengths[clip_id] for clip_id in clip_ids]
    sections = []
    result_list = []
    log_list = []
    for slot_index in range(2):
        triple = [
            spread_heads[slot_index, :, member].reshape(seq_len, head_count, HD)
            for member in range(3)
        ]
        results, log_totals = attend(
            triple[0],
            triple[1],
            triple[2],
            text_lens[slot_index],
            video_lens[slot_index],
            score_scale,
        )
        sections.append(triple)
        result_list.append(results)
        log_list.append(log_totals)
    attn_heads = jnp.stack(result_list).reshape(2, seq_len, 1, local_width)
    attn_back = lax.all_to_all(attn_heads, "seq", split_axis=1, concat_axis=2, tiled=True).reshape(
        2, row_count, head_width
    )
    outputs = jnp.einsum("crh,hd->crd", attn_back, out_weight, preferred_element_type=jnp.float32)
    mixed = (gate[:, None, :] * outputs).astype(jnp.bfloat16)
    gate_grad = taken_together(jnp.sum(cotangent.astype(jnp.float32) * outputs, axis=1), "seq")
    scaled = (cotangent.astype(jnp.float32) * gate[:, None, :]).astype(jnp.bfloat16)
    weight_rows = lax.dynamic_slice_in_dim(out_weight, seq_index * local_width, local_width, 0)
    flat_heads = attn_heads.reshape(2, seq_len, local_width)
    portion = lax.all_gather(scaled, "seq", axis=1, tiled=True)
    weight_part = jnp.einsum("cnh,cnd->hd", flat_heads, portion, preferred_element_type=jnp.float32)
    grad_rows = jnp.einsum(
        "cnd,hd->cnh", portion, weight_rows, preferred_element_type=jnp.float32
    ).astype(jnp.bfloat16)
    d_heads, weight_part = (grad_rows, weight_part)
    summed = lax.psum_scatter(weight_part, "dp", scatter_dimension=1, tiled=True)
    weight_grad = lax.all_to_all(summed, "seq", split_axis=1, concat_axis=0, tiled=True)
    grad_list = []
    for slot_index in range(2):
        triple = sections[slot_index]
        d_rows = d_heads[slot_index].reshape(seq_len, head_count, HD)
        grad_parts = attend_back(
            triple[0],
            triple[1],
            triple[2],
            result_list[slot_index],
            d_rows,
            log_list[slot_index],
            text_lens[slot_index],
            video_lens[slot_index],
            score_scale,
        )
        grad_list.append(
            jnp.stack([grad_part.reshape(seq_len, local_width) for grad_part in grad_parts], axis=1)
        )
    grad_heads = jnp.stack(grad_list).reshape(2, seq_len, 3, 1, local_width)
    grad_tokens = lax.all_to_all(
        grad_heads, "seq", split_axis=1, concat_axis=3, tiled=True
    ).reshape(2, row_count, 3 * head_width)
    grad_tokens = jnp.stack([grad_tokens[0], move_out(grad_tokens[1], plan)])
    return (mixed, gate_grad, weight_grad, grad_tokens)


def solution(mesh):
    in_specs = (P("dp", "seq", None), P("dp", None), P("dp", "seq", None), P(), P(), P(), P())
    out_specs = (P("dp", "seq", None), P("dp", None), P(None, ("dp", "seq")), P("dp", "seq", None))
    return jax.shard_map(body, mesh=mesh, in_specs=in_specs, out_specs=out_specs, check_vma=False)
```

profile of v0, /device:TPU:1, one launch (start us, length us, event | category | flops | bytes accessed | tf_op | source)
XLA Modules:
  0.0 709.6 jit_solution(8524687649885798854)
XLA Ops:
  7.2 4.9 fusion.183
  12.0 9.3 %all-to-all-start = ((bf16[32,8,4608]{2,1,0:T(8,128)(2,1)}), bf16[32,8,4608]{2,1,0:T(8,128)(2,1)S(1)}, u32[]{:S(2)}, u32[]{:S(2)}) async-start(bf16[32,8,4608]{2,1,0:T(8,128)(2,1)} %get-tuple-element.2898), calls=%async_computation | async-start | bytes 4718592 | tf_op jit(solution)/shard_map/all_to_all | solution.py:30
  21.5 30.6 %all-to-all-done = bf16[32,8,4608]{2,1,0:T(8,128)(2,1)S(1)} async-done(((bf16[32,8,4608]{2,1,0:T(8,128)(2,1)}), bf16[32,8,4608]{2,1,0:T(8,128)(2,1)S(1)}, u32[]{:S(2)}, u32[]{:S(2)}) %all-to-all-start) | async-done | bytes 2359328 | tf_op jit(solution)/shard_map/all_to_all | solution.py:30
  54.3 3.3 broadcast_select_fusion.1
  57.6 4.2 all-to-all-start.1
  61.9 4.3 copy.392
  66.1 25.9 %all-to-all-done.1 = bf16[32,8,4608]{2,1,0:T(8,128)(2,1)S(1)} async-done(((bf16[32,8,4608]{2,1,0:T(8,128)(2,1)}), bf16[32,8,4608]{2,1,0:T(8,128)(2,1)S(1)}, u32[]{:S(2)}, u32[]{:S(2)}) %all-to-all-start.1) | async-done | bytes 2359328 | tf_op jit(solution)/shard_map/all_to_all | solution.py:32
  94.1 5.5 copy.325
  104.3 8.3 %all-to-all-start.2 = ((bf16[2,256,3,4,384]{1,4,2,0,3:T(8,128)(2,1)}), bf16[2,256,3,4,384]{1,4,2,0,3:T(8,128)(2,1)}, u32[]{:S(2)}, u32[]{:S(2)}) async-start(bf16[2,256,3,4,384]{1,4,2,0,3:T(8,128)(2,1)} %copy.326), calls=%async_computation.2 | async-start | bytes 9437184 | tf_op jit(solution)/shard_map/all_to_all | solution.py:49
  117.0 49.8 %all-to-all-done.2 = bf16[2,256,3,4,384]{1,4,2,0,3:T(8,128)(2,1)} async-done(((bf16[2,256,3,4,384]{1,4,2,0,3:T(8,128)(2,1)}), bf16[2,256,3,4,384]{1,4,2,0,3:T(8,128)(2,1)}, u32[]{:S(2)}, u32[]{:S(2)}) %all-to-all-start.2) | async-done | bytes 4718624 | tf_op jit(solution)/shard_map/all_to_all | solution.py:49
  166.9 6.6 copy.327
  173.5 4.0 fusion.182
  181.5 25.5 %while.235 = (s32[]{:T(128)}, bf16[1024,3,128]{0,2,1:T(8,128)(2,1)S(1)}, f32[3,1024]{1,0:T(4,128)}, s32[]{:T(128)}, bf16[1024,3,128]{2,0,1:T(8,128)(2,1)}, /*ind...) while((s32[]{:T(128)}, ...), condition=%wide.region_16.18_spmd, body=%wide.region_9.17_spmd.sunk | while | flops 613564928 | bytes 14026645 | solution.py:118
  182.5 4.5 while.242
  187.8 6.3 while.243
  195.3 4.5 while.242
  200.5 6.3 while.243
  207.0 2.6 copy.328
  218.5 8.6 %while.232 = (s32[]{:T(128)}, bf16[1024,3,128]{0,2,1:T(8,128)(2,1)}, f32[3,1024]{1,0:T(4,128)}, s32[]{:T(128)}, bf16[1024,3,128]{2,0,1:T(8,128)(2,1)}, /*index=5...) while((s32[]{:T(128)}, bf16[1024,3,128]{0,2,1:T(8,128)(2,1)}, ...), condition=%wide.region_8.10_spmd, body=%wide.region_1.9_spmd.sunk | while | flops 613564928 | bytes 14026645 | solution.py:118
  223.0 3.2 while.241
  227.1 2.9 pad_maximum_fusion.2
  230.0 4.3 copy.338
  234.3 24.0 %all_to_all.89 = bf16[2,1024,1,384]{3,0,2,1:T(2,128)(2,1)S(1)} all-to-all(bf16[2,1024,1,384]{3,0,2,1:T(2,128)(2,1)S(1)} %copy.338), channel_id=1, replica_groups=mesh['dp'=32,'seq'=4] {'seq'}, dimensions={1} | all-to-all | bytes 3145728 | tf_op jit(solution)/shard_map/all_to_all | solution.py:229
  261.3 11.0 %fusion.166 = (f32[2,3072]{1,0:T(2,128)}, bf16[2,256,3072]{2,1,0:T(8,128)(2,1)}, bf16[2,256,3072]{2,1,0:T(8,128)(2,1)}) fusion(bf16[2,256,3072]{2,1,0:T(8,128)(2,1)} %param.31, f32[2,3072]{1,0:T(2,128)S(1)} %copy-done.29, bf16[2,256,1536]{2,1,0:T(8,128)(2,1)} %reshape.316, bf16[1536,3072]{1,0:T(8,128)(2,1)} %param.32), kind=kOutput, calls=%fused_computation.198 | convolution fusion | flops 4842842112 | bytes 20496384 | tf_op jit(solution)/shard_map/crh,hd->crd/dot_general | solution.py:232
  279.3 76.6 %all-gather.2.cloned.1.call-done = bf16[2,1024,3072]{2,1,0:T(8,128)(2,1)} async-done(((bf16[2,256,3072]{2,1,0:T(8,128)(2,1)}), bf16[2,1024,3072]{2,1,0:T(8,128)(2,1)}) %all-gather.2.cloned.1.call-update) | async-done | bytes 12582928 | tf_op jit(solution)/shard_map/all_gather | solution.py:238
  355.8 13.5 %fusion.171 = bf16[2,1024,384]{1,2,0:T(8,128)(2,1)S(1)} fusion(bf16[2,1024,3072]{2,1,0:T(8,128)(2,1)} %all-gather.2.cloned.1.call-done, bf16[1536,3072]{1,0:T(8,128)(2,1)} %param.32, s32[]{:T(128)S(6)} %select_n.154), kind=kOutput, calls=%fused_computation.213 | convolution fusion | flops 4832624640 | bytes 16515076 | tf_op jit(solution)/shard_map/cnd,hd->cnh/dot_general | solution.py:240
  374.0 36.1 %while.239 = (s32[]{:T(128)}, f32[1024,3,128]{0,2,1:T(8,128)}, f32[1024,3,128]{2,0,1:T(8,128)S(1)}, f32[1024,3,128]{2,0,1:T(8,128)}, s32[]{:T(128)}, /*index=5*/...) while((s32[]{:T(128)}, f32[1024,3,128]{0,2,1:T(8,128)}, ...), condition=%wide.region_27.29_spmd, body=%wide.region_24.28_spmd.sunk | while | flops 1015355392 | bytes 44485396 | solution.py:179
  378.0 13.3 %while.245 = (s32[]{:T(128)}, f32[512,3,128]{0,2,1:T(8,128)S(1)}, f32[1024,3,128]{2,0,1:T(8,128)S(1)}, f32[1024,3,128]{2,0,1:T(8,128)}, s32[]{:T(128)}, /*index=...) while((s32[]{:T(128)}, f32[512,3,128]{0,2,1:T(8,128)S(1)}, ...), condition=%wide.region_26.27_spmd.clone.clone, body=%wide.region_25.26_spmd.clone.clone.sunk | while | flops 1015355392 | bytes 39741808 | solution.py:174
  395.9 13.2 %while.245 = (s32[]{:T(128)}, f32[512,3,128]{0,2,1:T(8,128)S(1)}, f32[1024,3,128]{2,0,1:T(8,128)S(1)}, f32[1024,3,128]{2,0,1:T(8,128)}, s32[]{:T(128)}, /*index=...) while((s32[]{:T(128)}, f32[512,3,128]{0,2,1:T(8,128)S(1)}, ...), condition=%wide.region_26.27_spmd.clone.clone, body=%wide.region_25.26_spmd.clone.clone.sunk | while | flops 1015355392 | bytes 39741808 | solution.py:174
  422.9 11.4 %while.237 = (s32[]{:T(128)}, f32[1024,3,128]{0,2,1:T(8,128)}, f32[1024,3,128]{2,0,1:T(8,128)S(1)}, f32[1024,3,128]{2,0,1:T(8,128)}, s32[]{:T(128)}, /*index=5*/...) while((s32[]{:T(128)}, f32[1024,3,128]{0,2,1:T(8,128)}, ...), condition=%wide.region_23.25_spmd, body=%wide.region_20.24_spmd.sunk | while | flops 1015355392 | bytes 44485404 | solution.py:179
  426.7 6.7 while.244
  434.3 2.6 copy.353
  442.0 2.6 maximum_bitcast_fusion
  444.6 12.6 %copy.362 = bf16[2,1024,3,1,384]{4,0,3,2,1:T(2,128)(2,1)} copy(bf16[2,1024,3,1,384]{1,4,2,0,3:T(8,128)(2,1)} %maximum_bitcast_fusion) | data formatting | bytes 9437184 | tf_op jit(solution)/shard_map/reshape | solution.py:264
  457.3 5.5 all-to-all-start.6
  462.8 11.1 %convolution_bitcast_fusion.4 = f32[384,3072]{0,1:T(8,128)} fusion(bf16[2,1024,3072]{2,1,0:T(8,128)(2,1)} %all-gather.2.cloned.1.call-done, bf16[1,1024,384]{2,1,0:T(8,128)(2,1)S(1)} %copy-done.22, bf16[1,1024,384]{2,1,0:T(8,128)(2,1)S(1)} %copy-done.23), kind=kOutput, calls=%fused_computation.204 | convolution fusion | flops 4832624640 | bytes 18874368 | tf_op jit(solution)/shard_map/cnh,cnd->hd/dot_general | solution.py:239
  473.9 96.9 %all-to-all-done.6 = bf16[2,1024,3,1,384]{4,0,3,2,1:T(2,128)(2,1)} async-done(((bf16[2,1024,3,1,384]{4,0,3,2,1:T(2,128)(2,1)}), bf16[2,1024,3,1,384]{4,0,3,2,1:T(2,128)(2,1)}, u32[]{:S(2)}, u32[]{:S(2)}) %all-to-all-start.6) | async-done | bytes 4718624 | tf_op jit(solution)/shard_map/all_to_all | solution.py:265
  570.8 3.0 copy.363
  579.9 14.0 %all-to-all-start.7 = ((bf16[32,8,4608]{2,1,0:T(8,128)(2,1)}), bf16[32,8,4608]{2,1,0:T(8,128)(2,1)S(1)}, u32[]{:S(2)}, u32[]{:S(2)}) async-start(bf16[32,8,4608]{2,1,0:T(8,128)(2,1)} %reshape_squeeze.39), calls=%async_computation.8 | async-start | bytes 4718592 | tf_op jit(solution)/shard_map/all_to_all | solution.py:39
  593.9 28.4 %all-to-all-done.7 = bf16[32,8,4608]{2,1,0:T(8,128)(2,1)S(1)} async-done(((bf16[32,8,4608]{2,1,0:T(8,128)(2,1)}), bf16[32,8,4608]{2,1,0:T(8,128)(2,1)S(1)}, u32[]{:S(2)}, u32[]{:S(2)}) %all-to-all-start.7) | async-done | bytes 2359328 | tf_op jit(solution)/shard_map/all_to_all | solution.py:39
  622.9 9.2 %all-to-all-start.4 = ((f32[4,2,3072]{2,1,0:T(2,128)}), f32[4,2,3072]{2,1,0:T(2,128)S(1)}, u32[]{:S(2)}, u32[]{:S(2)}) async-start(f32[4,2,3072]{2,1,0:T(2,128)} %broadcast_in_dim.133), calls=%async_computation.4 | async-start | bytes 196608 | tf_op jit(solution)/shard_map/all_to_all | solution.py:14
  634.3 3.4 broadcast_select_fusion
  638.2 6.1 all-to-all-start.8
  645.0 4.3 copy.364
  649.3 25.0 %all-to-all-done.8 = bf16[32,8,4608]{2,1,0:T(8,128)(2,1)S(1)} async-done(((bf16[32,8,4608]{2,1,0:T(8,128)(2,1)}), bf16[32,8,4608]{2,1,0:T(8,128)(2,1)S(1)}, u32[]{:S(2)}, u32[]{:S(2)}) %all-to-all-start.8) | async-done | bytes 2359328 | tf_op jit(solution)/shard_map/all_to_all | solution.py:41
  676.8 13.5 %all-to-all-start.5 = ((f32[384,4,24]{0,2,1:T(8,128)}), f32[384,4,24]{0,2,1:T(8,128)S(1)}, u32[]{:S(2)}, u32[]{:S(2)}) async-start(f32[384,4,24]{0,2,1:T(8,128)} %bitcast.308), calls=%async_computation.6 | async-start | bytes 294912 | tf_op jit(solution)/shard_map/all_to_all | solution.py:245
  690.3 5.0 pad_maximum_fusion.1
  695.3 6.6 copy.367
  (276 shorter events, 150.7 us)
Async XLA Ops:
  12.0 9.4 %copy-start.30 = (s32[32]{0:T(128)S(1)}, s32[32]{0:T(128)}, u32[]{:S(2)}) copy-start(s32[32]{0:T(128)} %param.35) | copy-start | bytes 388
  12.0 40.1 %all-to-all-start = ((bf16[32,8,4608]{2,1,0:T(8,128)(2,1)}), bf16[32,8,4608]{2,1,0:T(8,128)(2,1)S(1)}, u32[]{:S(2)}, u32[]{:S(2)}) async-start(bf16[32,8,4608]{2,1,0:T(8,128)(2,1)} %get-tuple-element.2898), calls=%async_computation | async-start | bytes 4718592 | tf_op jit(solution)/shard_map/all_to_all | solution.py:30
  57.6 34.4 %all-to-all-start.1 = ((bf16[32,8,4608]{2,1,0:T(8,128)(2,1)}), bf16[32,8,4608]{2,1,0:T(8,128)(2,1)S(1)}, u32[]{:S(2)}, u32[]{:S(2)}) async-start(bf16[32,8,4608]{2,1,0:T(8,128)(2,1)} %broadcast_select_fusion.1), calls=%async_computation.1 | async-start | bytes 4718592 | tf_op jit(solution)/shard_map/all_to_all | solution.py:32
  94.1 5.5 copy-start.10
  104.3 9.5 %copy-start.27 = (s32[64]{0:T(128)S(1)}, s32[64]{0:T(128)}, u32[]{:S(2)}) copy-start(s32[64]{0:T(128)} %param.34) | copy-start | bytes 772
  104.3 9.5 %copy-start.28 = (s32[64]{0:T(128)S(1)}, s32[64]{0:T(128)}, u32[]{:S(2)}) copy-start(s32[64]{0:T(128)} %param.33) | copy-start | bytes 772
  104.3 62.6 %all-to-all-start.2 = ((bf16[2,256,3,4,384]{1,4,2,0,3:T(8,128)(2,1)}), bf16[2,256,3,4,384]{1,4,2,0,3:T(8,128)(2,1)}, u32[]{:S(2)}, u32[]{:S(2)}) async-start(bf16[2,256,3,4,384]{1,4,2,0,3:T(8,128)(2,1)} %copy.326), calls=%async_computation.2 | async-start | bytes 9437184 | tf_op jit(solution)/shard_map/all_to_all | solution.py:49
  112.5 243.3 %all-gather.2.cloned.1.call-start = ((), (), s32[]{:S(2)}) async-start(), calls=%async_computation.10 | async-start | bytes 15728640 | tf_op jit(solution)/shard_map/all_gather | solution.py:238
  207.0 6.1 copy-start.6
  207.0 4.9 copy-start.16
  227.1 7.3 %copy-start = (bf16[1024,3,128]{2,0,1:T(8,128)(2,1)}, bf16[1024,3,128]{2,0,1:T(8,128)(2,1)S(1)}, u32[]{:S(2)}) copy-start(bf16[1024,3,128]{2,0,1:T(8,128)(2,1)S(1)} %get-tuple-element.4344) | copy-start | bytes 2359300
  259.8 1.5 copy-start.29
  272.3 4.6 copy-start.7
  273.4 4.7 copy-start.4
  370.4 2.3 copy-start.3
  378.0 1.4 copy-start.8
  378.0 1.4 copy-start.25
  381.0 1.4 copy-start.11
  383.4 1.1 copy-start.12
  384.6 1.4 copy-start.8
  384.6 1.4 copy-start.25
  387.6 1.4 copy-start.11
  395.9 1.4 copy-start.8
  396.0 1.4 copy-start.25
  399.0 1.4 copy-start.11
  402.6 1.4 copy-start.8
  402.6 1.4 copy-start.25
  405.6 1.4 copy-start.11
  414.3 5.0 copy-start.2
  414.3 5.0 copy-start.5
  420.2 2.7 copy-start.1
  426.7 1.4 copy-start.9
  426.7 1.4 copy-start.24
  429.8 1.4 copy-start.14
  436.9 3.3 copy-start.13
  438.6 1.9 copy-start.18
  438.6 1.9 copy-start.19
  438.6 2.1 copy-start.20
  457.3 5.5 copy-start.22
  457.3 5.5 copy-start.23
  457.3 113.5 %all-to-all-start.6 = ((bf16[2,1024,3,1,384]{4,0,3,2,1:T(2,128)(2,1)}), bf16[2,1024,3,1,384]{4,0,3,2,1:T(2,128)(2,1)}, u32[]{:S(2)}, u32[]{:S(2)}) async-start(bf16[2,1024,3,1,384]{4,0,3,2,1:T(2,128)(2,1)} %copy.362), calls=%async_computation.7 | async-start | bytes 9437184 | tf_op jit(solution)/shard_map/all_to_all | solution.py:265
  462.8 214.0 %reduce-scatter.2.cloned.1.call-start = ((), (), s32[]{:S(2)}) async-start(), calls=%async_computation.11 | async-start | bytes 4866048 | tf_op jit(solution)/shard_map/reduce_scatter | solution.py:244
  579.9 14.0 %copy-start.31 = (s32[32]{0:T(128)S(1)}, s32[32]{0:T(128)}, u32[]{:S(2)}) copy-start(s32[32]{0:T(128)} %param.35) | copy-start | bytes 388
  579.9 42.4 %copy-start.26 = (f32[2,3072]{1,0:T(2,128)S(1)}, f32[2,3072]{1,0:T(2,128)}, u32[]{:S(2)}) copy-start(f32[2,3072]{1,0:T(2,128)} %get-tuple-element.2887) | copy-start | bytes 73732
  579.9 42.4 %all-to-all-start.7 = ((bf16[32,8,4608]{2,1,0:T(8,128)(2,1)}), bf16[32,8,4608]{2,1,0:T(8,128)(2,1)S(1)}, u32[]{:S(2)}, u32[]{:S(2)}) async-start(bf16[32,8,4608]{2,1,0:T(8,128)(2,1)} %reshape_squeeze.39), calls=%async_computation.8 | async-start | bytes 4718592 | tf_op jit(solution)/shard_map/all_to_all | solution.py:39
  622.9 15.3 %all-to-all-start.4 = ((f32[4,2,3072]{2,1,0:T(2,128)}), f32[4,2,3072]{2,1,0:T(2,128)S(1)}, u32[]{:S(2)}, u32[]{:S(2)}) async-start(f32[4,2,3072]{2,1,0:T(2,128)} %broadcast_in_dim.133), calls=%async_computation.4 | async-start | bytes 196608 | tf_op jit(solution)/shard_map/all_to_all | solution.py:14
  638.2 36.1 %all-to-all-start.8 = ((bf16[32,8,4608]{2,1,0:T(8,128)(2,1)}), bf16[32,8,4608]{2,1,0:T(8,128)(2,1)S(1)}, u32[]{:S(2)}, u32[]{:S(2)}) async-start(bf16[32,8,4608]{2,1,0:T(8,128)(2,1)} %broadcast_select_fusion), calls=%async_computation.9 | async-start | bytes 4718592 | tf_op jit(solution)/shard_map/all_to_all | solution.py:41
  676.8 25.1 %all-to-all-start.5 = ((f32[384,4,24]{0,2,1:T(8,128)}), f32[384,4,24]{0,2,1:T(8,128)S(1)}, u32[]{:S(2)}, u32[]{:S(2)}) async-start(f32[384,4,24]{0,2,1:T(8,128)} %bitcast.308), calls=%async_computation.6 | async-start | bytes 294912 | tf_op jit(solution)/shard_map/all_to_all | solution.py:245
  (6 other events, 6.9 us)
Sparse Core Ops, SparseCore 0:
  272.5 83.3 all-gather.1
  474.1 177.7 reduce-scatter.1
where the time goes:
time: 720 us; the launch traced here: 710 us
  waiting for transfers between devices  334 us (46%)
  local copies, waits for them, and re-layouts  144 us (20%)
  matrix products  70.4 us (10%)
  starting transfers between devices  70.2 us (10%)
  other arithmetic  47.2 us (7%)
  blocking collectives  24 us (3%)
  between operations  17.9 us (2%)
    all_to_all x1, waiting for transfers between devices, body(): lax.all_to_all(grad_heads, 'seq', split_axis=1, concat_axis=3, tiled=True)  96.9 us
    all_gather x1, waiting for transfers between devices, body(): portion = lax.all_gather(scaled, 'seq', axis=1, tiled=True)  76.6 us
    all_to_all x1, waiting for transfers between devices, to_heads(): lax.all_to_all(parted, 'seq', split_axis=3, concat_axis=1, tiled=True)  49.8 us
    all_to_all x1, waiting for transfers between devices, move_in(): lax.all_to_all(portions, 'dp', split_axis=0, concat_axis=0, tiled=True)  30.6 us
    all_to_all x1, waiting for transfers between devices, move_out(): lax.all_to_all(portions, 'dp', split_axis=0, concat_axis=0, tiled=True)  28.4 us
    all_to_all x1, waiting for transfers between devices, move_in(): lax.all_to_all(arranged, 'dp', split_axis=0, concat_axis=0, tiled=True)  25.9 us
    all_to_all x1, waiting for transfers between devices, move_out(): lax.all_to_all(arranged, 'dp', split_axis=0, concat_axis=0, tiled=True)  25 us
    all_to_all x1, blocking collectives, body(): lax.all_to_all(attn_heads, 'seq', split_axis=1, concat_axis=2, tiled=True)  24 us
  transfers between devices with their start and end apart: 10, of which 8 were waited for; matrix products, arithmetic and copies ran while one was open for 8% of the time, Pallas kernels for 0%

commit v1 on v0

--- a/solution.py
+++ b/solution.py
@@ -235,7 +235,7 @@
     scaled = (cotangent.astype(jnp.float32) * gate[:, None, :]).astype(jnp.bfloat16)
     weight_rows = lax.dynamic_slice_in_dim(out_weight, seq_index * local_width, local_width, 0)
     flat_heads = attn_heads.reshape(2, seq_len, local_width)
-    portion = lax.all_gather(scaled, "seq", axis=1, tiled=True)
+    portion = jnp.concatenate(lax.all_gather(scaled, "seq"), 1)
     weight_part = jnp.einsum("cnh,cnd->hd", flat_heads, portion, preferred_element_type=jnp.float32)
     grad_rows = jnp.einsum(
         "cnd,hd->cnh", portion, weight_rows, preferred_element_type=jnp.float32

time: 720 us -> 771 us (1.071)
  local copies, waits for them, and re-layouts: 144 us -> 181 us
  matrix products: 70.4 us -> 79 us
    reshape x0 -> x1, local copies, waits for them, and re-layouts: none -> 20.8 us  [body(): portion = jnp.concatenate(lax.all_gather(scaled, 'seq'), 1)]
    all_gather x0 -> x1, local copies, waits for them, and re-layouts: none -> 20.1 us  [body(): portion = jnp.concatenate(lax.all_gather(scaled, 'seq'), 1)]
    dot_general x10, matrix products: 6.44 us -> 14.8 us  [block_scores(): jnp.einsum('qhd,khd->hqk', query_rows, key_rows, preferred_element_type=j...]
where the time goes in v1:
time: 771 us; the launch traced here: 759 us
  waiting for transfers between devices  336 us (44%)
  local copies, waits for them, and re-layouts  181 us (23%)
  matrix products  79 us (10%)
  starting transfers between devices  71 us (9%)
  other arithmetic  48 us (6%)
  blocking collectives  24 us (3%)
  between operations  17.9 us (2%)
    all_to_all x1, waiting for transfers between devices, body(): lax.all_to_all(grad_heads, 'seq', split_axis=1, concat_axis=3, tiled=True)  95.4 us
    all_gather x1, waiting for transfers between devices, body(): portion = jnp.concatenate(lax.all_gather(scaled, 'seq'), 1)  74.8 us
    all_to_all x1, waiting for transfers between devices, to_heads(): lax.all_to_all(parted, 'seq', split_axis=3, concat_axis=1, tiled=True)  49.8 us
    all_to_all x1, waiting for transfers between devices, move_out(): lax.all_to_all(portions, 'dp', split_axis=0, concat_axis=0, tiled=True)  33.4 us
    all_to_all x1, waiting for transfers between devices, move_in(): lax.all_to_all(portions, 'dp', split_axis=0, concat_axis=0, tiled=True)  30.6 us
    all_to_all x1, waiting for transfers between devices, move_in(): lax.all_to_all(arranged, 'dp', split_axis=0, concat_axis=0, tiled=True)  25.9 us
    all_to_all x1, waiting for transfers between devices, move_out(): lax.all_to_all(arranged, 'dp', split_axis=0, concat_axis=0, tiled=True)  25.9 us
    all_to_all x1, blocking collectives, body(): lax.all_to_all(attn_heads, 'seq', split_axis=1, concat_axis=2, tiled=True)  24 us
  transfers between devices with their start and end apart: 10, of which 8 were waited for; matrix products, arithmetic and copies ran while one was open for 8% of the time, Pallas kernels for 0%

profile of v1, /device:TPU:1, one launch (start us, length us, event | category | flops | bytes accessed | tf_op | source)
XLA Modules:
  0.0 759.2 jit_solution(16811905118243594958)
XLA Ops:
  7.2 4.9 fusion.183
  12.0 9.3 %all-to-all-start = ((bf16[32,8,4608]{2,1,0:T(8,128)(2,1)}), bf16[32,8,4608]{2,1,0:T(8,128)(2,1)S(1)}, u32[]{:S(2)}, u32[]{:S(2)}) async-start(bf16[32,8,4608]{2,1,0:T(8,128)(2,1)} %get-tuple-element.2898), calls=%async_computation | async-start | bytes 4718592 | tf_op jit(solution)/shard_map/all_to_all | solution.py:30
  21.5 30.6 %all-to-all-done = bf16[32,8,4608]{2,1,0:T(8,128)(2,1)S(1)} async-done(((bf16[32,8,4608]{2,1,0:T(8,128)(2,1)}), bf16[32,8,4608]{2,1,0:T(8,128)(2,1)S(1)}, u32[]{:S(2)}, u32[]{:S(2)}) %all-to-all-start) | async-done | bytes 2359328 | tf_op jit(solution)/shard_map/all_to_all | solution.py:30
  54.3 3.3 broadcast_select_fusion.1
  57.6 4.2 all-to-all-start.1
  61.9 4.3 copy.400
  66.1 25.9 %all-to-all-done.1 = bf16[32,8,4608]{2,1,0:T(8,128)(2,1)S(1)} async-done(((bf16[32,8,4608]{2,1,0:T(8,128)(2,1)}), bf16[32,8,4608]{2,1,0:T(8,128)(2,1)S(1)}, u32[]{:S(2)}, u32[]{:S(2)}) %all-to-all-start.1) | async-done | bytes 2359328 | tf_op jit(solution)/shard_map/all_to_all | solution.py:32
  94.1 5.5 copy.332
  104.3 8.3 %all-to-all-start.2 = ((bf16[2,256,3,4,384]{1,4,2,0,3:T(8,128)(2,1)}), bf16[2,256,3,4,384]{1,4,2,0,3:T(8,128)(2,1)}, u32[]{:S(2)}, u32[]{:S(2)}) async-start(bf16[2,256,3,4,384]{1,4,2,0,3:T(8,128)(2,1)} %copy.333), calls=%async_computation.2 | async-start | bytes 9437184 | tf_op jit(solution)/shard_map/all_to_all | solution.py:49
  117.0 49.8 %all-to-all-done.2 = bf16[2,256,3,4,384]{1,4,2,0,3:T(8,128)(2,1)} async-done(((bf16[2,256,3,4,384]{1,4,2,0,3:T(8,128)(2,1)}), bf16[2,256,3,4,384]{1,4,2,0,3:T(8,128)(2,1)}, u32[]{:S(2)}, u32[]{:S(2)}) %all-to-all-start.2) | async-done | bytes 4718624 | tf_op jit(solution)/shard_map/all_to_all | solution.py:49
  166.9 6.6 copy.334
  173.5 4.0 fusion.182
  181.4 28.4 %while.235 = (s32[]{:T(128)}, bf16[1024,3,128]{0,2,1:T(8,128)(2,1)S(1)}, f32[3,1024]{1,0:T(4,128)}, s32[]{:T(128)}, bf16[1024,3,128]{2,0,1:T(8,128)(2,1)S(1)}, /...) while((s32[]{:T(128)}, ...), condition=%wide.region_16.18_spmd, body=%wide.region_9.17_spmd.sunk | while | flops 613564928 | bytes 14024597 | solution.py:118
  181.5 6.7 while.242
  188.9 6.7 while.243
  195.7 6.7 while.242
  203.1 6.7 while.243
  221.3 8.6 %while.232 = (s32[]{:T(128)}, bf16[1024,3,128]{0,2,1:T(8,128)(2,1)}, f32[3,1024]{1,0:T(4,128)}, s32[]{:T(128)}, bf16[1024,3,128]{2,0,1:T(8,128)(2,1)}, /*index=5...) while((s32[]{:T(128)}, bf16[1024,3,128]{0,2,1:T(8,128)(2,1)}, ...), condition=%wide.region_8.10_spmd, body=%wide.region_1.9_spmd.sunk | while | flops 613564928 | bytes 14026645 | solution.py:118
  225.8 3.2 while.241
  229.9 2.9 pad_maximum_fusion.2
  232.9 4.3 copy.345
  237.2 24.0 %all_to_all.89 = bf16[2,1024,1,384]{3,0,2,1:T(2,128)(2,1)S(1)} all-to-all(bf16[2,1024,1,384]{3,0,2,1:T(2,128)(2,1)S(1)} %copy.345), channel_id=1, replica_groups=mesh['dp'=32,'seq'=4] {'seq'}, dimensions={1} | all-to-all | bytes 3145728 | tf_op jit(solution)/shard_map/all_to_all | solution.py:229
  264.2 11.0 %fusion.166 = (f32[2,3072]{1,0:T(2,128)}, bf16[2,256,3072]{2,1,0:T(8,128)(2,1)}, bf16[2,256,3072]{2,1,0:T(8,128)(2,1)}) fusion(bf16[2,256,3072]{2,1,0:T(8,128)(2,1)} %param.31, f32[2,3072]{1,0:T(2,128)S(1)} %copy-done.29, bf16[2,256,1536]{2,1,0:T(8,128)(2,1)} %reshape.322, bf16[1536,3072]{1,0:T(8,128)(2,1)} %param.32), kind=kOutput, calls=%fused_computation.198 | convolution fusion | flops 4842842112 | bytes 20496384 | tf_op jit(solution)/shard_map/crh,hd->crd/dot_general | solution.py:232
  282.1 74.8 %all-gather.3.cloned.1.call-done = bf16[8,256,3072]{2,1,0:T(8,128)(2,1)} async-done(((bf16[2,256,3072]{2,1,0:T(8,128)(2,1)}), bf16[8,256,3072]{2,1,0:T(8,128)(2,1)}) %all-gather.3.cloned.1.call-update) | async-done | bytes 12582928 | tf_op jit(solution)/shard_map/all_gather | solution.py:238
  356.9 20.1 %copy.351 = bf16[4,2,256,3072]{2,0,3,1:T(4,128)(2,1)} copy(bf16[4,2,256,3072]{3,2,1,0:T(8,128)(2,1)} %bitcast.292) | data formatting | bytes 25165824 | tf_op jit(solution)/shard_map/all_gather | solution.py:238
  377.0 20.8 %reshape.324 = bf16[2,1024,3072]{1,2,0:T(8,128)(2,1)} reshape(bf16[2,4,256,3072]{2,1,3,0:T(4,128)(2,1)} %bitcast.285) | data formatting | bytes 25165824 | tf_op jit(solution)/shard_map/reshape | solution.py:238
  397.8 8.7 %fusion.171 = bf16[2,1024,384]{1,2,0:T(8,128)(2,1)S(1)} fusion(bf16[2,1024,3072]{1,2,0:T(8,128)(2,1)} %reshape.324, bf16[1536,3072]{1,0:T(8,128)(2,1)} %param.32, s32[]{:T(128)S(6)} %select_n.154), kind=kOutput, calls=%fused_computation.213 | convolution fusion | flops 4832624640 | bytes 16515076 | tf_op jit(solution)/shard_map/cnd,hd->cnh/dot_general | solution.py:240
  411.2 42.7 %while.239 = (s32[]{:T(128)}, f32[1024,3,128]{0,2,1:T(8,128)}, f32[1024,3,128]{2,0,1:T(8,128)S(1)}, f32[1024,3,128]{2,0,1:T(8,128)}, s32[]{:T(128)}, /*index=5*/...) while((s32[]{:T(128)}, f32[1024,3,128]{0,2,1:T(8,128)}, ...), condition=%wide.region_27.29_spmd, body=%wide.region_24.28_spmd.sunk | while | flops 1015355392 | bytes 44485396 | solution.py:179
  414.2 17.5 %while.245 = (s32[]{:T(128)}, f32[512,3,128]{0,2,1:T(8,128)S(1)}, f32[1024,3,128]{2,0,1:T(8,128)S(1)}, f32[1024,3,128]{2,0,1:T(8,128)}, s32[]{:T(128)}, /*index=...) while((s32[]{:T(128)}, f32[512,3,128]{0,2,1:T(8,128)S(1)}, ...), condition=%wide.region_26.27_spmd.clone.clone, body=%wide.region_25.26_spmd.clone.clone.sunk | while | flops 1015355392 | bytes 39741808 | solution.py:174
  435.5 17.5 %while.245 = (s32[]{:T(128)}, f32[512,3,128]{0,2,1:T(8,128)S(1)}, f32[1024,3,128]{2,0,1:T(8,128)S(1)}, f32[1024,3,128]{2,0,1:T(8,128)}, s32[]{:T(128)}, /*index=...) while((s32[]{:T(128)}, f32[512,3,128]{0,2,1:T(8,128)S(1)}, ...), condition=%wide.region_26.27_spmd.clone.clone, body=%wide.region_25.26_spmd.clone.clone.sunk | while | flops 1015355392 | bytes 39741808 | solution.py:174
  466.7 11.4 %while.237 = (s32[]{:T(128)}, f32[1024,3,128]{0,2,1:T(8,128)}, f32[1024,3,128]{2,0,1:T(8,128)S(1)}, f32[1024,3,128]{2,0,1:T(8,128)}, s32[]{:T(128)}, /*index=5*/...) while((s32[]{:T(128)}, f32[1024,3,128]{0,2,1:T(8,128)}, ...), condition=%wide.region_23.25_spmd, body=%wide.region_20.24_spmd.sunk | while | flops 1015355392 | bytes 44485404 | solution.py:179
  470.5 6.7 while.244
  485.8 2.6 maximum_bitcast_fusion
  488.4 12.6 %copy.370 = bf16[2,1024,3,1,384]{4,0,3,2,1:T(2,128)(2,1)} copy(bf16[2,1024,3,1,384]{1,4,2,0,3:T(8,128)(2,1)} %maximum_bitcast_fusion) | data formatting | bytes 9437184 | tf_op jit(solution)/shard_map/reshape | solution.py:264
  501.1 5.5 all-to-all-start.6
  506.5 11.9 %convolution_bitcast_fusion.4 = f32[384,3072]{0,1:T(8,128)} fusion(bf16[2,1024,3072]{1,2,0:T(8,128)(2,1)} %reshape.324, bf16[1,1024,384]{2,1,0:T(8,128)(2,1)S(1)} %copy-done.22, bf16[1,1024,384]{2,1,0:T(8,128)(2,1)S(1)} %copy-done.23), kind=kOutput, calls=%fused_computation.204 | convolution fusion | flops 4832624640 | bytes 18874368 | tf_op jit(solution)/shard_map/cnh,cnd->hd/dot_general | solution.py:239
  518.4 95.4 %all-to-all-done.6 = bf16[2,1024,3,1,384]{4,0,3,2,1:T(2,128)(2,1)} async-done(((bf16[2,1024,3,1,384]{4,0,3,2,1:T(2,128)(2,1)}), bf16[2,1024,3,1,384]{4,0,3,2,1:T(2,128)(2,1)}, u32[]{:S(2)}, u32[]{:S(2)}) %all-to-all-start.6) | async-done | bytes 4718624 | tf_op jit(solution)/shard_map/all_to_all | solution.py:265
  613.9 3.0 copy.371
  623.0 13.3 %all-to-all-start.7 = ((bf16[32,8,4608]{2,1,0:T(8,128)(2,1)}), bf16[32,8,4608]{2,1,0:T(8,128)(2,1)S(1)}, u32[]{:S(2)}, u32[]{:S(2)}) async-start(bf16[32,8,4608]{2,1,0:T(8,128)(2,1)} %reshape_squeeze.39), calls=%async_computation.8 | async-start | bytes 4718592 | tf_op jit(solution)/shard_map/all_to_all | solution.py:39
  636.3 33.4 %all-to-all-done.7 = bf16[32,8,4608]{2,1,0:T(8,128)(2,1)S(1)} async-done(((bf16[32,8,4608]{2,1,0:T(8,128)(2,1)}), bf16[32,8,4608]{2,1,0:T(8,128)(2,1)S(1)}, u32[]{:S(2)}, u32[]{:S(2)}) %all-to-all-start.7) | async-done | bytes 2359328 | tf_op jit(solution)/shard_map/all_to_all | solution.py:39
  670.4 4.3 all-to-all-start.4
  676.9 3.4 broadcast_select_fusion
  680.6 5.7 all-to-all-start.8
  686.9 4.3 copy.372
  691.2 25.9 %all-to-all-done.8 = bf16[32,8,4608]{2,1,0:T(8,128)(2,1)S(1)} async-done(((bf16[32,8,4608]{2,1,0:T(8,128)(2,1)}), bf16[32,8,4608]{2,1,0:T(8,128)(2,1)S(1)}, u32[]{:S(2)}, u32[]{:S(2)}) %all-to-all-start.8) | async-done | bytes 2359328 | tf_op jit(solution)/shard_map/all_to_all | solution.py:41
  719.6 20.4 %all-to-all-start.5 = ((f32[384,4,24]{0,2,1:T(8,128)}), f32[384,4,24]{0,2,1:T(8,128)S(1)}, u32[]{:S(2)}, u32[]{:S(2)}) async-start(f32[384,4,24]{0,2,1:T(8,128)} %bitcast.314), calls=%async_computation.6 | async-start | bytes 294912 | tf_op jit(solution)/shard_map/all_to_all | solution.py:245
  739.9 5.0 pad_maximum_fusion.1
  744.9 6.6 copy.375
  (278 shorter events, 165.1 us)
Async XLA Ops:
  12.0 9.4 %copy-start.30 = (s32[32]{0:T(128)S(1)}, s32[32]{0:T(128)}, u32[]{:S(2)}) copy-start(s32[32]{0:T(128)} %param.35) | copy-start | bytes 388
  12.0 40.1 %all-to-all-start = ((bf16[32,8,4608]{2,1,0:T(8,128)(2,1)}), bf16[32,8,4608]{2,1,0:T(8,128)(2,1)S(1)}, u32[]{:S(2)}, u32[]{:S(2)}) async-start(bf16[32,8,4608]{2,1,0:T(8,128)(2,1)} %get-tuple-element.2898), calls=%async_computation | async-start | bytes 4718592 | tf_op jit(solution)/shard_map/all_to_all | solution.py:30
  57.6 34.4 %all-to-all-start.1 = ((bf16[32,8,4608]{2,1,0:T(8,128)(2,1)}), bf16[32,8,4608]{2,1,0:T(8,128)(2,1)S(1)}, u32[]{:S(2)}, u32[]{:S(2)}) async-start(bf16[32,8,4608]{2,1,0:T(8,128)(2,1)} %broadcast_select_fusion.1), calls=%async_computation.1 | async-start | bytes 4718592 | tf_op jit(solution)/shard_map/all_to_all | solution.py:32
  94.1 5.5 copy-start.10
  104.3 9.5 %copy-start.27 = (s32[64]{0:T(128)S(1)}, s32[64]{0:T(128)}, u32[]{:S(2)}) copy-start(s32[64]{0:T(128)} %param.34) | copy-start | bytes 772
  104.3 9.5 %copy-start.28 = (s32[64]{0:T(128)S(1)}, s32[64]{0:T(128)}, u32[]{:S(2)}) copy-start(s32[64]{0:T(128)} %param.33) | copy-start | bytes 772
  104.3 62.6 %all-to-all-start.2 = ((bf16[2,256,3,4,384]{1,4,2,0,3:T(8,128)(2,1)}), bf16[2,256,3,4,384]{1,4,2,0,3:T(8,128)(2,1)}, u32[]{:S(2)}, u32[]{:S(2)}) async-start(bf16[2,256,3,4,384]{1,4,2,0,3:T(8,128)(2,1)} %copy.333), calls=%async_computation.2 | async-start | bytes 9437184 | tf_op jit(solution)/shard_map/all_to_all | solution.py:49
  112.5 244.4 %all-gather.3.cloned.1.call-start = ((), (), s32[]{:S(2)}) async-start(), calls=%async_computation.11 | async-start | bytes 15728640 | tf_op jit(solution)/shard_map/all_gather | solution.py:238
  209.8 6.1 copy-start.6
  209.8 4.9 copy-start.16
  229.9 7.3 copy-start
  262.6 1.5 copy-start.29
  275.2 4.6 copy-start.7
  276.3 4.7 copy-start.4
  407.6 2.4 copy-start.3
  414.2 2.5 copy-start.8
  414.2 2.5 copy-start.25
  419.4 1.4 copy-start.11
  421.8 1.1 copy-start.12
  423.0 2.5 copy-start.8
  423.0 2.5 copy-start.25
  428.1 1.4 copy-start.11
  435.5 2.5 copy-start.8
  435.5 2.5 copy-start.25
  440.6 1.4 copy-start.11
  444.2 2.5 copy-start.8
  444.2 2.5 copy-start.25
  449.4 1.4 copy-start.11
  458.1 5.0 copy-start.2
  458.1 5.0 copy-start.5
  464.0 2.7 copy-start.1
  470.5 1.4 copy-start.9
  470.5 1.4 copy-start.24
  473.6 1.4 copy-start.14
  480.7 3.3 copy-start.13
  482.3 1.9 copy-start.18
  482.3 1.9 copy-start.19
  482.3 2.1 copy-start.20
  501.0 5.5 copy-start.22
  501.1 5.5 copy-start.23
  501.1 112.8 %all-to-all-start.6 = ((bf16[2,1024,3,1,384]{4,0,3,2,1:T(2,128)(2,1)}), bf16[2,1024,3,1,384]{4,0,3,2,1:T(2,128)(2,1)}, u32[]{:S(2)}, u32[]{:S(2)}) async-start(bf16[2,1024,3,1,384]{4,0,3,2,1:T(2,128)(2,1)} %copy.370), calls=%async_computation.7 | async-start | bytes 9437184 | tf_op jit(solution)/shard_map/all_to_all | solution.py:265
  506.5 213.0 %reduce-scatter.2.cloned.1.call-start = ((), (), s32[]{:S(2)}) async-start(), calls=%async_computation.10 | async-start | bytes 4866048 | tf_op jit(solution)/shard_map/reduce_scatter | solution.py:244
  623.0 13.3 %copy-start.31 = (s32[32]{0:T(128)S(1)}, s32[32]{0:T(128)}, u32[]{:S(2)}) copy-start(s32[32]{0:T(128)} %param.35) | copy-start | bytes 388
  623.0 46.8 %copy-start.26 = (f32[2,3072]{1,0:T(2,128)S(1)}, f32[2,3072]{1,0:T(2,128)}, u32[]{:S(2)}) copy-start(f32[2,3072]{1,0:T(2,128)} %get-tuple-element.2887) | copy-start | bytes 73732
  623.0 46.8 %all-to-all-start.7 = ((bf16[32,8,4608]{2,1,0:T(8,128)(2,1)}), bf16[32,8,4608]{2,1,0:T(8,128)(2,1)S(1)}, u32[]{:S(2)}, u32[]{:S(2)}) async-start(bf16[32,8,4608]{2,1,0:T(8,128)(2,1)} %reshape_squeeze.39), calls=%async_computation.8 | async-start | bytes 4718592 | tf_op jit(solution)/shard_map/all_to_all | solution.py:39
  670.4 10.2 %all-to-all-start.4 = ((f32[4,2,3072]{2,1,0:T(2,128)}), f32[4,2,3072]{2,1,0:T(2,128)S(1)}, u32[]{:S(2)}, u32[]{:S(2)}) async-start(f32[4,2,3072]{2,1,0:T(2,128)} %broadcast_in_dim.133), calls=%async_computation.4 | async-start | bytes 196608 | tf_op jit(solution)/shard_map/all_to_all | solution.py:14
  680.6 36.4 %all-to-all-start.8 = ((bf16[32,8,4608]{2,1,0:T(8,128)(2,1)}), bf16[32,8,4608]{2,1,0:T(8,128)(2,1)S(1)}, u32[]{:S(2)}, u32[]{:S(2)}) async-start(bf16[32,8,4608]{2,1,0:T(8,128)(2,1)} %broadcast_select_fusion), calls=%async_computation.9 | async-start | bytes 4718592 | tf_op jit(solution)/shard_map/all_to_all | solution.py:41
  719.6 31.9 %all-to-all-start.5 = ((f32[384,4,24]{0,2,1:T(8,128)}), f32[384,4,24]{0,2,1:T(8,128)S(1)}, u32[]{:S(2)}, u32[]{:S(2)}) async-start(f32[384,4,24]{0,2,1:T(8,128)} %bitcast.314), calls=%async_computation.6 | async-start | bytes 294912 | tf_op jit(solution)/shard_map/all_to_all | solution.py:245
  (6 other events, 6.9 us)
Sparse Core Ops, SparseCore 0:
  275.3 81.5 all-gather.2
  518.6 180.9 reduce-scatter.1
